TPU v7x, 32 devices: a whole 2x2x4 slice. The times are simulated.
32 devices in a mesh: tm: 4 (over z), mem: 4 (over y, x), tile: 2 (over core).
Axes of the slice: x: 2, y: 2, z: 4, core: 2. Of those that a mesh axis runs over, the one named last changes fastest.
Arguments:
- control: float32 [40, 2, 8, 256], P('mem', None, 'tile'), may hold values from -6 to 6
- vertical_modes: float32 [64, 2], replicated, may hold values from -4 to 4
- mode_counts: int32 [8], P('tile'), may hold values from 1 to 2, as said below
- perturbations: bfloat16 [40, 8, 64, 8, 256], P('mem', 'tm', None, 'tile'), may hold values from -6 to 6
- slot_index: int32 [12], P('tm'), may hold values from 0 to 7, as said below
- blend_weight: float32 [12], P('tm'), may hold values from 0 to 1
Outputs:
- increment: float32 [12, 64, 8, 256], P('tm', None, 'tile')
Inputs may be any that keep to these rules, and one draw needn't show every extreme that they name: slot_index[w] // 2 == w // 3. `mode_counts`: both ends of the range occur.
All inputs are finite; a program needn't handle non-finite values.
Results may differ from a plain program's by a relative error of at most 0.0003.
Values sent between devices are 32-bit elements; how exact they have to be, the bound alone decides.
No kernel may reach another device: no remote copies, remote signals or barrier semaphores. Data moves between devices by JAX's collectives and lax.ppermute only.
A program may use at most 64 MiB of HBM per device.

v0:
```python
import math
import jax
import jax.numpy as jnp
from jax import lax
from jax.sharding import PartitionSpec as P

VM = 2
SMOOTH = 4
diffusion = 0.24


def ring(count, shift):
    return [(i, (i + shift) % count) for i in range(count)]


def is_power(count):
    return count & count - 1 == 0


def pairing(count, step):
    if is_power(count):
        return [(i, i ^ step) for i in range(count)]
    return ring(count, step)


def target_of(place, count, step):
    if is_power(count):
        return place ^ step
    return (place + step) % count


def source_of(place, count, step):
    if is_power(count):
        return place ^ step
    return (place - step) % count


def relax(field):
    neighbours = jnp.roll(field, -1, axis=2) + jnp.roll(field, 1, axis=2)
    bordered = jnp.pad(field, ((0, 0), (0, 0), (0, 0), (1, 1)))
    lateral = bordered[:, :, :, 2:] + bordered[:, :, :, :-2]
    return field + diffusion * (neighbours + lateral - 4.0 * field)


def smooth(field):
    count = lax.axis_size("tile")
    width = field.shape[2]
    left = SMOOTH
    while left:
        reach = min(left, width)
        if count == 1:
            wide, start = (field, 0)
        elif count == 2 and reach == width:
            other = lax.ppermute(field, "tile", ring(2, 1))
            wide, start = (jnp.concatenate([field, other], axis=2), 0)
        else:
            head = lax.slice_in_dim(field, 0, reach, axis=2)
            tail = lax.slice_in_dim(field, width - reach, width, axis=2)
            before = lax.ppermute(tail, "tile", ring(count, 1))
            after = lax.ppermute(head, "tile", ring(count, -1))
            wide, start = (jnp.concatenate([before, field, after], axis=2), reach)
        for _ in range(reach):
            wide = relax(wide)
        field = lax.slice_in_dim(wide, start, start + width, axis=2)
        left -= reach
    return field


def per_device(control, vertical_modes, mode_counts, perturbations, slot_index, blend_weight):
    members, slot_count, levels = perturbations.shape[:3]
    group = lax.axis_size("mem")
    place = lax.axis_index("mem")
    share = levels // group
    norm_factor = 1.0 / math.sqrt(members * group - 1)
    field = smooth(control)
    masked = []
    for mode_index in range(VM):
        keep_mode = (mode_index < mode_counts).astype(jnp.float32)
        masked.append(keep_mode[None, :, None] * field[:, mode_index])

    def terms(owner):
        part = lax.dynamic_slice_in_dim(perturbations, owner * share, share, axis=2)
        modes = lax.dynamic_slice_in_dim(vertical_modes, owner * share, share, axis=0)
        localized = sum((modes[:, m][None, :, None, None] * masked[m][:, None] for m in range(VM)))
        return jnp.sum(localized[:, None] * part.astype(jnp.float32), axis=0)

    arrived = []
    for step in range(group - 1, 0, -1):
        arrived.append(
            lax.ppermute(terms(target_of(place, group, step)), "mem", pairing(group, step))
        )
    slots = terms(place)
    for part in arrived:
        slots = slots + part
    slots = slots * norm_factor
    stages = lax.axis_size("tm")
    stage = lax.axis_index("tm")
    total = jnp.sum(slots, axis=0)
    earlier = jnp.zeros_like(total)
    for step in range(1, stages):
        came = lax.ppermute(total, "tm", ring(stages, step))
        earlier = earlier + jnp.where(stage >= step, came, 0.0)
    local_slot = slot_index - stage * slot_count
    blended = []
    for w in range(slot_index.shape[0]):
        mixed = earlier
        for s in range(slot_count):
            factor = jnp.where(
                local_slot[w] == s, blend_weight[w], jnp.where(local_slot[w] > s, 1.0, 0.0)
            )
            mixed = mixed + factor * slots[s]
        blended.append(mixed)
    blended = jnp.stack(blended)
    return lax.all_gather(blended, "mem", axis=1, tiled=True)


def solution(mesh):
    placed = (
        P("mem", None, "tile", None),
        P(),
        P("tile"),
        P("mem", "tm", None, "tile", None),
        P("tm"),
        P("tm"),
    )
    return jax.shard_map(
        per_device,
        mesh=mesh,
        in_specs=placed,
        out_specs=P("tm", None, "tile", None),
        check_vma=False,
    )
```

profile of v0, /device:TPU:0, one launch (start us, length us, event | category | flops | bytes accessed | tf_op | source)
XLA Modules:
  0.0 44.2 jit_solution(4025381710863709894)
XLA Ops:
  0.0 0.5 %collective-permute-start = (f32[10,2,4,256]{3,2,1,0:T(4,128)}, f32[10,2,4,256]{3,2,1,0:T(4,128)S(1)}, u32[]{:S(2)}, u32[]{:S(2)}) collective-permute-start(f32[10,2,4,256]{3,2,1,0:T(4,128)} %param.6), channel_id=1, source_target_pairs={{0,1},{1,0},{2,3},{3,2},{4,5},{5,4},{6,7},{7,6},{8,9},{9,8},{10,11... | collective-permute-start | bytes 245768 | tf_op jit(solution)/shard_map/ppermute | solution.py:54
  0.5 0.9 %constant_dynamic-slice_fusion.1 = (f32[16,2]{0,1:T(2,128)S(1)}, f32[16,2]{0,1:T(2,128)S(1)}, f32[16,2]{0,1:T(2,128)S(1)}, f32[16,2]{0,1:T(2,128)S(1)}) fusion(f32[64,2]{0,1:T(2,128)} %param.7, s32[]{:T(128)S(6)} %select_n.101, s32[]{:T(128)S(6)} %select_n.100, s32[]{:T(128)S(6)} %select_n.99, s32[]{:T(128)S(6)} %select_n.102), kind=kLoop, calls=%fused_computation.64 | loop fusion | bytes 1040 | tf_op jit(solution)/shard_map/dynamic_slice | solution.py:83
  1.4 0.7 %compare_convert_fusion.1 = (f32[4]{0:T(128)S(1)}, f32[4]{0:T(128)S(1)}) fusion(s32[4]{0:T(128)} %param.8), kind=kLoop, calls=%fused_computation.68 | loop fusion | flops 16 | bytes 48 | tf_op jit(solution)/shard_map/convert_element_type | solution.py:78
  2.1 0.9 %slice.153 = f32[10,2,1,256]{3,2,1,0:T(1,128)S(1)} slice(f32[10,2,4,256]{3,2,1,0:T(4,128)} %param.6), slice={[0:10], [0:2], [0:1], [0:256]} | slice | bytes 40960 | tf_op jit(solution)/shard_map/jit(_roll_static)/slice | solution.py:39
  3.0 1.0 %fusion.1 = (f32[10,2,7,256]{3,2,1,0:T(8,128)S(1)}, f32[10,2,7,256]{3,2,1,0:T(8,128)S(1)}) fusion(f32[10,2,4,256]{3,2,1,0:T(4,128)} %param.6, f32[10,2,4,256]{3,2,1,0:T(4,128)S(1)} %collective-permute-done), kind=kLoop, calls=%fused_computation.23 | loop fusion | flops 71680 | bytes 450560 | tf_op jit(solution)/shard_map/concatenate | solution.py:55
  4.0 0.9 %pad_maximum_fusion = f32[10,2,8,256]{3,2,1,0:T(8,128)S(1)} fusion(f32[10,2,4,256]{3,2,1,0:T(4,128)S(1)} %collective-permute-done, f32[10,2,4,256]{3,2,1,0:T(4,128)} %param.6), kind=kLoop, calls=%fused_computation.18 | loop fusion | flops 40960 | bytes 327680 | tf_op jit(solution)/shard_map/concatenate | solution.py:55
  5.0 0.2 fusion.6
  5.2 0.2 fusion.11
  5.5 0.2 fusion.16
  5.7 0.2 fusion.21
  6.0 0.8 %multiply_add_fusion.1 = (f32[10,16,4,256]{3,2,1,0:T(4,128)S(1)}, f32[10,16,4,256]{3,2,1,0:T(4,128)S(1)}, f32[10,16,4,256]{3,2,1,0:T(4,128)S(1)}, f32[10,16,4,256]{3,2,1,0:T(4,128)S(1)}) fusion(f32[16]{0:T(128)S(1)} %get-tuple-element.55, f32[16]{0:T(128)S(1)} %get-tuple-element.56, f32[10,4,256]{2,1,0:T(4,128)S(1)} %get-tuple-element.16, ...), kind=kLoop, calls=%fused_computation.5 | loop fusion | flops 1966080 | bytes 2703872 | tf_op jit(solution)/shard_map/add | solution.py:84
  6.7 1.0 %copy-done = bf16[10,2,64,4,256]{4,3,2,1,0:T(4,128)(2,1)S(1)} copy-done((bf16[10,2,64,4,256]{4,3,2,1,0:T(4,128)(2,1)S(1)}, bf16[10,2,64,4,256]{4,3,2,1,0:T(4,128)(2,1)}, u32[]{:S(2)}) %copy-start) | copy-done | bytes 2621464
  7.7 1.5 %multiply_reduce_fusion.2 = (f32[2,16,4,256]{3,2,1,0:T(4,128)S(1)}, f32[2,16,4,256]{3,2,1,0:T(4,128)S(1)}, f32[2,16,4,256]{3,2,1,0:T(4,128)S(1)}, f32[2,16,4,256]{3,2,1,0:T(4,128)S(1)}) fusion(bf16[10,2,64,4,256]{4,3,2,1,0:T(4,128)(2,1)S(1)} %copy-done, s32[]{:T(128)S(6)} %select_n.100, f32[10,16,4,256]{3,2,1,0:T(4,128)S(1)} %get-tuple-element.32, ...), kind=kLoop, calls=%fused_computation.2 | loop fusion | flops 3801088 | bytes 5767184 | tf_op jit(solution)/shard_map/reduce_sum | solution.py:85
  9.2 3.5 %collective-permute-start.1 = (f32[2,16,4,256]{3,2,1,0:T(4,128)S(1)}, f32[2,16,4,256]{3,2,1,0:T(4,128)S(1)}, u32[]{:S(2)}, u32[]{:S(2)}) collective-permute-start(f32[2,16,4,256]{3,2,1,0:T(4,128)S(1)} %get-tuple-element.5), channel_id=1, source_target_pairs={{0,6},{2,4},{4,2},{6,0},{1,7},{3,5},{5,3},{7,1},{8,14},{10,12},{12... | collective-permute-start | bytes 393224 | tf_op jit(solution)/shard_map/ppermute | solution.py:90
  12.7 0.5 %collective-permute-start.2 = (f32[2,16,4,256]{3,2,1,0:T(4,128)S(1)}, f32[2,16,4,256]{3,2,1,0:T(4,128)S(1)}, u32[]{:S(2)}, u32[]{:S(2)}) collective-permute-start(f32[2,16,4,256]{3,2,1,0:T(4,128)S(1)} %get-tuple-element.8), channel_id=1, source_target_pairs={{0,4},{2,6},{4,0},{6,2},{1,5},{3,7},{5,1},{7,3},{8,12},{10,14},{12... | collective-permute-start | bytes 393224 | tf_op jit(solution)/shard_map/ppermute | solution.py:90
  13.2 0.1 collective-permute-start.3
  13.4 0.7 %fusion.35 = (s32[1]{0:T(128)}, s32[1]{0:T(128)}, s32[1]{0:T(128)}) fusion(s32[3]{0:T(128)S(1)} %broadcast_subtract_fusion), kind=kLoop, calls=%fused_computation.86 | loop fusion | bytes 24 | tf_op jit(solution)/shard_map/slice | solution.py:109
  21.7 0.1 fusion.27
  21.8 2.0 %collective-permute-start.4 = (f32[16,4,256]{2,1,0:T(4,128)S(1)}, f32[16,4,256]{2,1,0:T(4,128)S(1)}, u32[]{:S(2)}, u32[]{:S(2)}) collective-permute-start(f32[16,4,256]{2,1,0:T(4,128)S(1)} %get-tuple-element.11), channel_id=1, source_target_pairs={{0,8},{8,16},{16,24},{24,0},{1,9},{9,17},{17,25},{25,1},{2,10},{10... | collective-permute-start | bytes 196616 | tf_op jit(solution)/shard_map/ppermute | solution.py:101
  23.8 2.6 %collective-permute-start.5 = (f32[16,4,256]{2,1,0:T(4,128)S(1)}, f32[16,4,256]{2,1,0:T(4,128)S(1)}, u32[]{:S(2)}, u32[]{:S(2)}) collective-permute-start(f32[16,4,256]{2,1,0:T(4,128)S(1)} %get-tuple-element.11), channel_id=1, source_target_pairs={{0,16},{8,24},{16,0},{24,8},{1,17},{9,25},{17,1},{25,9},{2,18},{10... | collective-permute-start | bytes 196616 | tf_op jit(solution)/shard_map/ppermute | solution.py:101
  26.4 1.3 %collective-permute-start.6 = (f32[16,4,256]{2,1,0:T(4,128)S(1)}, f32[16,4,256]{2,1,0:T(4,128)S(1)}, u32[]{:S(2)}, u32[]{:S(2)}) collective-permute-start(f32[16,4,256]{2,1,0:T(4,128)S(1)} %get-tuple-element.11), channel_id=1, source_target_pairs={{0,24},{8,0},{16,8},{24,16},{1,25},{9,1},{17,9},{25,17},{2,26},{10... | collective-permute-start | bytes 196616 | tf_op jit(solution)/shard_map/ppermute | solution.py:101
  27.8 0.6 %fusion.34 = (f32[1]{0:T(128)}, f32[1]{0:T(128)}, f32[1]{0:T(128)}) fusion(f32[3]{0:T(128)S(1)} %copy-done.1), kind=kLoop, calls=%fused_computation.85 | loop fusion | bytes 24 | tf_op jit(solution)/shard_map/slice | solution.py:109
  32.2 11.1 %all_gather.3 = f32[3,64,4,256]{3,2,1,0:T(4,128)S(1)} all-gather(f32[3,16,4,256]{3,2,1,0:T(4,128)S(1)} %pad_maximum_fusion.1), channel_id=1, replica_groups=mesh['tm'=4,'mem'=4,'tile'=2] {'mem'}, dimensions={1}, use_global_device_ids=true | all-gather | bytes 983040 | tf_op jit(solution)/shard_map/all_gather | solution.py:114
  43.4 0.9 %copy.8 = f32[3,64,4,256]{3,2,1,0:T(4,128)} copy(f32[3,64,4,256]{3,2,1,0:T(4,128)S(1)} %all_gather.3) | data formatting | bytes 1572864
  (26 shorter events, 0.5 us)
Async XLA Ops:
  0.0 3.0 %collective-permute-start = (f32[10,2,4,256]{3,2,1,0:T(4,128)}, f32[10,2,4,256]{3,2,1,0:T(4,128)S(1)}, u32[]{:S(2)}, u32[]{:S(2)}) collective-permute-start(f32[10,2,4,256]{3,2,1,0:T(4,128)} %param.6), channel_id=1, source_target_pairs={{0,1},{1,0},{2,3},{3,2},{4,5},{5,4},{6,7},{7,6},{8,9},{9,8},{10,11... | collective-permute-start | bytes 245768 | tf_op jit(solution)/shard_map/ppermute | solution.py:54
  5.9 1.7 %copy-start = (bf16[10,2,64,4,256]{4,3,2,1,0:T(4,128)(2,1)S(1)}, bf16[10,2,64,4,256]{4,3,2,1,0:T(4,128)(2,1)}, u32[]{:S(2)}) copy-start(bf16[10,2,64,4,256]{4,3,2,1,0:T(4,128)(2,1)} %param.9) | copy-start | bytes 7864324
  7.7 5.7 %copy-start.2 = (s32[3]{0:T(128)S(1)}, s32[3]{0:T(128)}, u32[]{:S(2)}) copy-start(s32[3]{0:T(128)} %param.10) | copy-start | bytes 40
  7.7 20.1 %copy-start.1 = (f32[3]{0:T(128)S(1)}, f32[3]{0:T(128)}, u32[]{:S(2)}) copy-start(f32[3]{0:T(128)} %param.11) | copy-start | bytes 40
  9.2 12.4 %collective-permute-start.1 = (f32[2,16,4,256]{3,2,1,0:T(4,128)S(1)}, f32[2,16,4,256]{3,2,1,0:T(4,128)S(1)}, u32[]{:S(2)}, u32[]{:S(2)}) collective-permute-start(f32[2,16,4,256]{3,2,1,0:T(4,128)S(1)} %get-tuple-element.5), channel_id=1, source_target_pairs={{0,6},{2,4},{4,2},{6,0},{1,7},{3,5},{5,3},{7,1},{8,14},{10,12},{12... | collective-permute-start | bytes 393224 | tf_op jit(solution)/shard_map/ppermute | solution.py:90
  12.7 8.9 %collective-permute-start.2 = (f32[2,16,4,256]{3,2,1,0:T(4,128)S(1)}, f32[2,16,4,256]{3,2,1,0:T(4,128)S(1)}, u32[]{:S(2)}, u32[]{:S(2)}) collective-permute-start(f32[2,16,4,256]{3,2,1,0:T(4,128)S(1)} %get-tuple-element.8), channel_id=1, source_target_pairs={{0,4},{2,6},{4,0},{6,2},{1,5},{3,7},{5,1},{7,3},{8,12},{10,14},{12... | collective-permute-start | bytes 393224 | tf_op jit(solution)/shard_map/ppermute | solution.py:90
  13.2 8.4 %collective-permute-start.3 = (f32[2,16,4,256]{3,2,1,0:T(4,128)S(1)}, f32[2,16,4,256]{3,2,1,0:T(4,128)S(1)}, u32[]{:S(2)}, u32[]{:S(2)}) collective-permute-start(f32[2,16,4,256]{3,2,1,0:T(4,128)S(1)} %get-tuple-element.7), channel_id=1, source_target_pairs={{0,2},{2,0},{4,6},{6,4},{1,3},{3,1},{5,7},{7,5},{8,10},{10,8},{12,... | collective-permute-start | bytes 393224 | tf_op jit(solution)/shard_map/ppermute | solution.py:90
  21.8 10.2 %collective-permute-start.4 = (f32[16,4,256]{2,1,0:T(4,128)S(1)}, f32[16,4,256]{2,1,0:T(4,128)S(1)}, u32[]{:S(2)}, u32[]{:S(2)}) collective-permute-start(f32[16,4,256]{2,1,0:T(4,128)S(1)} %get-tuple-element.11), channel_id=1, source_target_pairs={{0,8},{8,16},{16,24},{24,0},{1,9},{9,17},{17,25},{25,1},{2,10},{10... | collective-permute-start | bytes 196616 | tf_op jit(solution)/shard_map/ppermute | solution.py:101
  23.8 8.2 %collective-permute-start.5 = (f32[16,4,256]{2,1,0:T(4,128)S(1)}, f32[16,4,256]{2,1,0:T(4,128)S(1)}, u32[]{:S(2)}, u32[]{:S(2)}) collective-permute-start(f32[16,4,256]{2,1,0:T(4,128)S(1)} %get-tuple-element.11), channel_id=1, source_target_pairs={{0,16},{8,24},{16,0},{24,8},{1,17},{9,25},{17,1},{25,9},{2,18},{10... | collective-permute-start | bytes 196616 | tf_op jit(solution)/shard_map/ppermute | solution.py:101
  26.4 5.6 %collective-permute-start.6 = (f32[16,4,256]{2,1,0:T(4,128)S(1)}, f32[16,4,256]{2,1,0:T(4,128)S(1)}, u32[]{:S(2)}, u32[]{:S(2)}) collective-permute-start(f32[16,4,256]{2,1,0:T(4,128)S(1)} %get-tuple-element.11), channel_id=1, source_target_pairs={{0,24},{8,0},{16,8},{24,16},{1,25},{9,1},{17,9},{25,17},{2,26},{10... | collective-permute-start | bytes 196616 | tf_op jit(solution)/shard_map/ppermute | solution.py:101
where the time goes:
time: 44.7 us; the launch traced here: 44.2 us
  between operations  11.5 us (26%)
  blocking collectives  11.1 us (25%)
  starting transfers between devices  10.6 us (24%)
  other arithmetic  5.92 us (13%)
  local copies, waits for them, and re-layouts  5.11 us (11%)
    all_gather x1, blocking collectives, per_device(): return lax.all_gather(blended, 'mem', axis=1, tiled=True)  11.1 us
    ppermute x3, starting transfers between devices, per_device(): came = lax.ppermute(total, 'tm', ring(stages, step))  5.97 us
    ppermute x3, starting transfers between devices, per_device(): lax.ppermute(terms(target_of(place, group, step)), 'mem', pairing(group,...  4.14 us
    concatenate x2, other arithmetic, smooth(): wide, start = (jnp.concatenate([field, other], axis=2), 0)  1.96 us
    unnamed x7, local copies, waits for them, and re-layouts  1.85 us
    reduce_sum x1, other arithmetic, terms(): return jnp.sum(localized[:, None] * part.astype(jnp.float32), axis=0)  1.54 us
    slice x8, local copies, waits for them, and re-layouts, relax(): neighbours = jnp.roll(field, -1, axis=2) + jnp.roll(field, 1, axis=2)  1.08 us
    dynamic_slice x1, local copies, waits for them, and re-layouts, terms(): lax.dynamic_slice_in_dim(vertical_modes, owner * share, share, axis=0)  0.9 us
  transfers between devices with their start and end apart: 7, of which 0 were waited for; matrix products, arithmetic and copies ran while one was open for 8% of the time, Pallas kernels for 0%

commit v1 on v0

--- a/solution.py
+++ b/solution.py
@@ -7,6 +7,13 @@
 VM = 2
 SMOOTH = 4
 diffusion = 0.24
+
+
+def gather_over(x, axis, d):
+    n_dev = lax.axis_size(axis)
+    shards = jnp.stack([x for _ in range(n_dev)])
+    shards = lax.all_to_all(shards, axis, split_axis=0, concat_axis=0)
+    return jnp.concatenate(shards, axis=d)
 
 
 def ring(count, shift):
@@ -111,7 +118,7 @@
             mixed = mixed + factor * slots[s]
         blended.append(mixed)
     blended = jnp.stack(blended)
-    return lax.all_gather(blended, "mem", axis=1, tiled=True)
+    return gather_over(blended, "mem", 1)
 
 
 def solution(mesh):

time: 44.7 us -> 48.2 us (1.078)
  blocking collectives: 11.1 us -> 13.8 us
  local copies, waits for them, and re-layouts: 5.11 us -> 5.89 us
    all_to_all x0 -> x1, blocking collectives: none -> 13.8 us  [gather_over(): shards = lax.all_to_all(shards, axis, split_axis=0, concat_axis=0)]
    all_gather x1 -> x0, blocking collectives: 11.1 us -> none  [per_device(): return lax.all_gather(blended, 'mem', axis=1, tiled=True)]
    reshape x0 -> x1, local copies, waits for them, and re-layouts: none -> 1.39 us  [gather_over(): return jnp.concatenate(shards, axis=d)]
    unnamed x7 -> x6, local copies, waits for them, and re-layouts: 1.85 us -> 0.97 us
where the time goes in v1:
time: 48.2 us; the launch traced here: 47.7 us
  blocking collectives  13.8 us (29%)
  between operations  11.5 us (24%)
  starting transfers between devices  10.6 us (22%)
  other arithmetic  5.92 us (12%)
  local copies, waits for them, and re-layouts  5.89 us (12%)
    all_to_all x1, blocking collectives, gather_over(): shards = lax.all_to_all(shards, axis, split_axis=0, concat_axis=0)  13.8 us
    ppermute x3, starting transfers between devices, per_device(): came = lax.ppermute(total, 'tm', ring(stages, step))  5.97 us
    ppermute x3, starting transfers between devices, per_device(): lax.ppermute(terms(target_of(place, group, step)), 'mem', pairing(group,...  4.14 us
    concatenate x2, other arithmetic, smooth(): wide, start = (jnp.concatenate([field, other], axis=2), 0)  1.96 us
    reduce_sum x1, other arithmetic, terms(): return jnp.sum(localized[:, None] * part.astype(jnp.float32), axis=0)  1.54 us
    reshape x1, local copies, waits for them, and re-layouts, gather_over(): return jnp.concatenate(shards, axis=d)  1.39 us
    slice x8, local copies, waits for them, and re-layouts, relax(): neighbours = jnp.roll(field, -1, axis=2) + jnp.roll(field, 1, axis=2)  1.08 us
    unnamed x6, local copies, waits for them, and re-layouts  0.97 us
  transfers between devices with their start and end apart: 7, of which 0 were waited for; matrix products, arithmetic and copies ran while one was open for 8% of the time, Pallas kernels for 0%

profile of v1, /device:TPU:0, one launch (start us, length us, event | category | flops | bytes accessed | tf_op | source)
XLA Modules:
  0.0 47.7 jit_solution(12814436466504905702)
XLA Ops:
  0.0 0.5 %collective-permute-start = (f32[10,2,4,256]{3,2,1,0:T(4,128)}, f32[10,2,4,256]{3,2,1,0:T(4,128)S(1)}, u32[]{:S(2)}, u32[]{:S(2)}) collective-permute-start(f32[10,2,4,256]{3,2,1,0:T(4,128)} %param.6), channel_id=1, source_target_pairs={{0,1},{1,0},{2,3},{3,2},{4,5},{5,4},{6,7},{7,6},{8,9},{9,8},{10,11... | collective-permute-start | bytes 245768 | tf_op jit(solution)/shard_map/ppermute | solution.py:61
  0.5 0.9 %constant_dynamic-slice_fusion.1 = (f32[16,2]{0,1:T(2,128)S(1)}, f32[16,2]{0,1:T(2,128)S(1)}, f32[16,2]{0,1:T(2,128)S(1)}, f32[16,2]{0,1:T(2,128)S(1)}) fusion(f32[64,2]{0,1:T(2,128)} %param.7, s32[]{:T(128)S(6)} %select_n.101, s32[]{:T(128)S(6)} %select_n.100, s32[]{:T(128)S(6)} %select_n.99, s32[]{:T(128)S(6)} %select_n.102), kind=kLoop, calls=%fused_computation.64 | loop fusion | bytes 1040 | tf_op jit(solution)/shard_map/dynamic_slice | solution.py:90
  1.4 0.7 %compare_convert_fusion.1 = (f32[4]{0:T(128)S(1)}, f32[4]{0:T(128)S(1)}) fusion(s32[4]{0:T(128)} %param.8), kind=kLoop, calls=%fused_computation.68 | loop fusion | flops 16 | bytes 48 | tf_op jit(solution)/shard_map/convert_element_type | solution.py:85
  2.1 0.9 %slice.153 = f32[10,2,1,256]{3,2,1,0:T(1,128)S(1)} slice(f32[10,2,4,256]{3,2,1,0:T(4,128)} %param.6), slice={[0:10], [0:2], [0:1], [0:256]} | slice | bytes 40960 | tf_op jit(solution)/shard_map/jit(_roll_static)/slice | solution.py:46
  3.0 1.0 %fusion.1 = (f32[10,2,7,256]{3,2,1,0:T(8,128)S(1)}, f32[10,2,7,256]{3,2,1,0:T(8,128)S(1)}) fusion(f32[10,2,4,256]{3,2,1,0:T(4,128)} %param.6, f32[10,2,4,256]{3,2,1,0:T(4,128)S(1)} %collective-permute-done), kind=kLoop, calls=%fused_computation.23 | loop fusion | flops 71680 | bytes 450560 | tf_op jit(solution)/shard_map/concatenate | solution.py:62
  4.0 0.9 %pad_maximum_fusion = f32[10,2,8,256]{3,2,1,0:T(8,128)S(1)} fusion(f32[10,2,4,256]{3,2,1,0:T(4,128)S(1)} %collective-permute-done, f32[10,2,4,256]{3,2,1,0:T(4,128)} %param.6), kind=kLoop, calls=%fused_computation.18 | loop fusion | flops 40960 | bytes 327680 | tf_op jit(solution)/shard_map/concatenate | solution.py:62
  5.0 0.2 fusion.6
  5.2 0.2 fusion.11
  5.5 0.2 fusion.16
  5.7 0.2 fusion.21
  6.0 0.8 %multiply_add_fusion.1 = (f32[10,16,4,256]{3,2,1,0:T(4,128)S(1)}, f32[10,16,4,256]{3,2,1,0:T(4,128)S(1)}, f32[10,16,4,256]{3,2,1,0:T(4,128)S(1)}, f32[10,16,4,256]{3,2,1,0:T(4,128)S(1)}) fusion(f32[16]{0:T(128)S(1)} %get-tuple-element.55, f32[16]{0:T(128)S(1)} %get-tuple-element.56, f32[10,4,256]{2,1,0:T(4,128)S(1)} %get-tuple-element.16, ...), kind=kLoop, calls=%fused_computation.5 | loop fusion | flops 1966080 | bytes 2703872 | tf_op jit(solution)/shard_map/add | solution.py:91
  6.7 1.0 %copy-done = bf16[10,2,64,4,256]{4,3,2,1,0:T(4,128)(2,1)S(1)} copy-done((bf16[10,2,64,4,256]{4,3,2,1,0:T(4,128)(2,1)S(1)}, bf16[10,2,64,4,256]{4,3,2,1,0:T(4,128)(2,1)}, u32[]{:S(2)}) %copy-start) | copy-done | bytes 2621464
  7.7 1.5 %multiply_reduce_fusion.2 = (f32[2,16,4,256]{3,2,1,0:T(4,128)S(1)}, f32[2,16,4,256]{3,2,1,0:T(4,128)S(1)}, f32[2,16,4,256]{3,2,1,0:T(4,128)S(1)}, f32[2,16,4,256]{3,2,1,0:T(4,128)S(1)}) fusion(bf16[10,2,64,4,256]{4,3,2,1,0:T(4,128)(2,1)S(1)} %copy-done, s32[]{:T(128)S(6)} %select_n.100, f32[10,16,4,256]{3,2,1,0:T(4,128)S(1)} %get-tuple-element.32, ...), kind=kLoop, calls=%fused_computation.2 | loop fusion | flops 3801088 | bytes 5767184 | tf_op jit(solution)/shard_map/reduce_sum | solution.py:92
  9.2 3.5 %collective-permute-start.1 = (f32[2,16,4,256]{3,2,1,0:T(4,128)S(1)}, f32[2,16,4,256]{3,2,1,0:T(4,128)S(1)}, u32[]{:S(2)}, u32[]{:S(2)}) collective-permute-start(f32[2,16,4,256]{3,2,1,0:T(4,128)S(1)} %get-tuple-element.5), channel_id=1, source_target_pairs={{0,6},{2,4},{4,2},{6,0},{1,7},{3,5},{5,3},{7,1},{8,14},{10,12},{12... | collective-permute-start | bytes 393224 | tf_op jit(solution)/shard_map/ppermute | solution.py:97
  12.7 0.5 %collective-permute-start.2 = (f32[2,16,4,256]{3,2,1,0:T(4,128)S(1)}, f32[2,16,4,256]{3,2,1,0:T(4,128)S(1)}, u32[]{:S(2)}, u32[]{:S(2)}) collective-permute-start(f32[2,16,4,256]{3,2,1,0:T(4,128)S(1)} %get-tuple-element.8), channel_id=1, source_target_pairs={{0,4},{2,6},{4,0},{6,2},{1,5},{3,7},{5,1},{7,3},{8,12},{10,14},{12... | collective-permute-start | bytes 393224 | tf_op jit(solution)/shard_map/ppermute | solution.py:97
  13.2 0.1 collective-permute-start.3
  13.4 0.7 %fusion.35 = (s32[1]{0:T(128)}, s32[1]{0:T(128)}, s32[1]{0:T(128)}) fusion(s32[3]{0:T(128)S(1)} %broadcast_subtract_fusion), kind=kLoop, calls=%fused_computation.86 | loop fusion | bytes 24 | tf_op jit(solution)/shard_map/slice | solution.py:116
  21.8 2.0 %collective-permute-start.4 = (f32[16,4,256]{2,1,0:T(4,128)S(1)}, f32[16,4,256]{2,1,0:T(4,128)S(1)}, u32[]{:S(2)}, u32[]{:S(2)}) collective-permute-start(f32[16,4,256]{2,1,0:T(4,128)S(1)} %get-tuple-element.11), channel_id=1, source_target_pairs={{0,8},{8,16},{16,24},{24,0},{1,9},{9,17},{17,25},{25,1},{2,10},{10... | collective-permute-start | bytes 196616 | tf_op jit(solution)/shard_map/ppermute | solution.py:108
  23.8 2.6 %collective-permute-start.5 = (f32[16,4,256]{2,1,0:T(4,128)S(1)}, f32[16,4,256]{2,1,0:T(4,128)S(1)}, u32[]{:S(2)}, u32[]{:S(2)}) collective-permute-start(f32[16,4,256]{2,1,0:T(4,128)S(1)} %get-tuple-element.11), channel_id=1, source_target_pairs={{0,16},{8,24},{16,0},{24,8},{1,17},{9,25},{17,1},{25,9},{2,18},{10... | collective-permute-start | bytes 196616 | tf_op jit(solution)/shard_map/ppermute | solution.py:108
  26.4 1.3 %collective-permute-start.6 = (f32[16,4,256]{2,1,0:T(4,128)S(1)}, f32[16,4,256]{2,1,0:T(4,128)S(1)}, u32[]{:S(2)}, u32[]{:S(2)}) collective-permute-start(f32[16,4,256]{2,1,0:T(4,128)S(1)} %get-tuple-element.11), channel_id=1, source_target_pairs={{0,24},{8,0},{16,8},{24,16},{1,25},{9,1},{17,9},{25,17},{2,26},{10... | collective-permute-start | bytes 196616 | tf_op jit(solution)/shard_map/ppermute | solution.py:108
  27.8 0.6 %fusion.34 = (f32[1]{0:T(128)}, f32[1]{0:T(128)}, f32[1]{0:T(128)}) fusion(f32[3]{0:T(128)S(1)} %copy-done.1), kind=kLoop, calls=%fused_computation.85 | loop fusion | bytes 24 | tf_op jit(solution)/shard_map/slice | solution.py:116
  32.4 13.8 %all_to_all.5 = f32[4,3,16,4,256]{4,3,2,1,0:T(4,128)S(1)} all-to-all(f32[4,3,16,4,256]{4,3,2,1,0:T(4,128)S(1)} %stack.23), channel_id=1, replica_groups=mesh['tm'=4,'mem'=4,'tile'=2] {'mem'}, dimensions={0} | all-to-all | bytes 1572864 | tf_op jit(solution)/shard_map/all_to_all | solution.py:15
  46.2 0.1 copy.7
  46.3 1.4 %copy.8 = f32[3,64,4,256]{3,2,1,0:T(4,128)} copy(f32[3,64,4,256]{3,1,2,0:T(8,128)S(1)} %bitcast.59) | data formatting | bytes 1572864 | tf_op jit(solution)/shard_map/reshape | solution.py:16
  (28 shorter events, 0.7 us)
Async XLA Ops:
  0.0 3.0 %collective-permute-start = (f32[10,2,4,256]{3,2,1,0:T(4,128)}, f32[10,2,4,256]{3,2,1,0:T(4,128)S(1)}, u32[]{:S(2)}, u32[]{:S(2)}) collective-permute-start(f32[10,2,4,256]{3,2,1,0:T(4,128)} %param.6), channel_id=1, source_target_pairs={{0,1},{1,0},{2,3},{3,2},{4,5},{5,4},{6,7},{7,6},{8,9},{9,8},{10,11... | collective-permute-start | bytes 245768 | tf_op jit(solution)/shard_map/ppermute | solution.py:61
  5.9 1.7 %copy-start = (bf16[10,2,64,4,256]{4,3,2,1,0:T(4,128)(2,1)S(1)}, bf16[10,2,64,4,256]{4,3,2,1,0:T(4,128)(2,1)}, u32[]{:S(2)}) copy-start(bf16[10,2,64,4,256]{4,3,2,1,0:T(4,128)(2,1)} %param.9) | copy-start | bytes 7864324
  7.7 5.7 %copy-start.2 = (s32[3]{0:T(128)S(1)}, s32[3]{0:T(128)}, u32[]{:S(2)}) copy-start(s32[3]{0:T(128)} %param.10) | copy-start | bytes 40
  7.7 20.1 %copy-start.1 = (f32[3]{0:T(128)S(1)}, f32[3]{0:T(128)}, u32[]{:S(2)}) copy-start(f32[3]{0:T(128)} %param.11) | copy-start | bytes 40
  9.2 12.4 %collective-permute-start.1 = (f32[2,16,4,256]{3,2,1,0:T(4,128)S(1)}, f32[2,16,4,256]{3,2,1,0:T(4,128)S(1)}, u32[]{:S(2)}, u32[]{:S(2)}) collective-permute-start(f32[2,16,4,256]{3,2,1,0:T(4,128)S(1)} %get-tuple-element.5), channel_id=1, source_target_pairs={{0,6},{2,4},{4,2},{6,0},{1,7},{3,5},{5,3},{7,1},{8,14},{10,12},{12... | collective-permute-start | bytes 393224 | tf_op jit(solution)/shard_map/ppermute | solution.py:97
  12.7 8.9 %collective-permute-start.2 = (f32[2,16,4,256]{3,2,1,0:T(4,128)S(1)}, f32[2,16,4,256]{3,2,1,0:T(4,128)S(1)}, u32[]{:S(2)}, u32[]{:S(2)}) collective-permute-start(f32[2,16,4,256]{3,2,1,0:T(4,128)S(1)} %get-tuple-element.8), channel_id=1, source_target_pairs={{0,4},{2,6},{4,0},{6,2},{1,5},{3,7},{5,1},{7,3},{8,12},{10,14},{12... | collective-permute-start | bytes 393224 | tf_op jit(solution)/shard_map/ppermute | solution.py:97
  13.2 8.4 %collective-permute-start.3 = (f32[2,16,4,256]{3,2,1,0:T(4,128)S(1)}, f32[2,16,4,256]{3,2,1,0:T(4,128)S(1)}, u32[]{:S(2)}, u32[]{:S(2)}) collective-permute-start(f32[2,16,4,256]{3,2,1,0:T(4,128)S(1)} %get-tuple-element.7), channel_id=1, source_target_pairs={{0,2},{2,0},{4,6},{6,4},{1,3},{3,1},{5,7},{7,5},{8,10},{10,8},{12,... | collective-permute-start | bytes 393224 | tf_op jit(solution)/shard_map/ppermute | solution.py:97
  21.8 10.2 %collective-permute-start.4 = (f32[16,4,256]{2,1,0:T(4,128)S(1)}, f32[16,4,256]{2,1,0:T(4,128)S(1)}, u32[]{:S(2)}, u32[]{:S(2)}) collective-permute-start(f32[16,4,256]{2,1,0:T(4,128)S(1)} %get-tuple-element.11), channel_id=1, source_target_pairs={{0,8},{8,16},{16,24},{24,0},{1,9},{9,17},{17,25},{25,1},{2,10},{10... | collective-permute-start | bytes 196616 | tf_op jit(solution)/shard_map/ppermute | solution.py:108
  23.8 8.2 %collective-permute-start.5 = (f32[16,4,256]{2,1,0:T(4,128)S(1)}, f32[16,4,256]{2,1,0:T(4,128)S(1)}, u32[]{:S(2)}, u32[]{:S(2)}) collective-permute-start(f32[16,4,256]{2,1,0:T(4,128)S(1)} %get-tuple-element.11), channel_id=1, source_target_pairs={{0,16},{8,24},{16,0},{24,8},{1,17},{9,25},{17,1},{25,9},{2,18},{10... | collective-permute-start | bytes 196616 | tf_op jit(solution)/shard_map/ppermute | solution.py:108
  26.4 5.6 %collective-permute-start.6 = (f32[16,4,256]{2,1,0:T(4,128)S(1)}, f32[16,4,256]{2,1,0:T(4,128)S(1)}, u32[]{:S(2)}, u32[]{:S(2)}) collective-permute-start(f32[16,4,256]{2,1,0:T(4,128)S(1)} %get-tuple-element.11), channel_id=1, source_target_pairs={{0,24},{8,0},{16,8},{24,16},{1,25},{9,1},{17,9},{25,17},{2,26},{10... | collective-permute-start | bytes 196616 | tf_op jit(solution)/shard_map/ppermute | solution.py:108
